TPU v7x, 64 devices: a 2x2x8 block of a 4x4x8 slice. The times are simulated.
64 devices in a mesh: dp: 4 (over x, y), tp: 16 (over z, core).
Axes of the slice: x: 2, y: 2, z: 8, core: 2. Of those that a mesh axis runs over, the one named last changes fastest.
The devices are a block of a 4x4x8 slice.
Arguments:
- x_tokens: bfloat16 [8192, 2048], P(('dp', 'tp')), parts along dimension 0
- dy_tokens: bfloat16 [8192, 2048], P(('dp', 'tp')), parts along dimension 0
- w_q: bfloat16 [2048, 16, 128], P(None, 'tp')
- w_k: bfloat16 [2048, 2, 128], replicated
- w_v: bfloat16 [2048, 2, 128], replicated
- w_o: bfloat16 [16, 128, 2048], P('tp')
- w_gate: bfloat16 [2048, 11008], P(None, 'tp')
- w_up: bfloat16 [2048, 11008], P(None, 'tp')
- w_down: bfloat16 [11008, 2048], P('tp')
Outputs:
- output 1: bfloat16 [8192, 2048], P(('dp', 'tp')), parts along dimension 0
- output 2: float32 [8192, 16, 128], P('dp', 'tp'), parts along dimension 0
- output 3: float32 [64, 256, 128], P(('dp', 'tp')), parts along dimension 0
- output 4: float32 [64, 256, 128], P(('dp', 'tp')), parts along dimension 0
- output 5: float32 [64, 128, 2048], P(('dp', 'tp')), parts along dimension 0
- output 6: float32 [8192, 11008], P('dp', 'tp'), parts along dimension 0
- output 7: float32 [8192, 11008], P('dp', 'tp'), parts along dimension 0
- output 8: float32 [44032, 2048], P(('dp', 'tp')), parts along dimension 0
There are 4 independent parts. A program takes and returns all parts, laid end to end along the dimension named above; an argument that names none is the same for every part.
All inputs are finite; a program needn't handle non-finite values.
Results may differ from a plain program's by a relative error of at most 0.0166535.
Values are sent between devices in bfloat16 or wider.
A program may use at most 768 MiB of HBM per device.

v0:
```python
import functools

import jax
import jax.numpy as jnp
from jax import lax
from jax.experimental import pallas as pl
from jax.experimental.pallas import tpu as pltpu
from jax.sharding import PartitionSpec as P

MESH = pl.DeviceIdType.MESH
BF = jnp.bfloat16
F32 = jnp.float32
SUBS = 2


def dot_nt(a, b):
    return lax.dot_general(a, b, (((1,), (1,)), ((), ())), preferred_element_type=F32)


def dot_tn(a, b):
    return lax.dot_general(a, b, (((0,), (0,)), ((), ())), preferred_element_type=F32)


def dot_nn(a, b):
    return jnp.dot(a, b, preferred_element_type=F32)


class Sizes:
    def __init__(self, n_dev, kv_count, tok, d_model, ff, hd):
        self.n, self.kv, self.tok, self.d, self.ff, self.hd = n_dev, kv_count, tok, d_model, ff, hd
        self.chips = n_dev // 2
        self.seq = n_dev * tok
        self.fm = (ff // 128) * 128
        self.ft = ff - self.fm
        assert 0 < 2 * self.ft <= 128 and self.ft % 16 == 0 and hd == 128 and tok == 128
        self.au, self.aq, self.ak, self.av = self.fm, 2 * self.fm, 2 * self.fm + hd, 2 * self.fm + 2 * hd
        self.at = 2 * self.fm + 3 * hd
        self.wa = self.at + 128
        self.yo, self.yt = self.fm, self.fm + hd
        self.wy = self.yt + 128
        self.pair = 2 * tok


def fused_kernel(z_, x_hbm, y_hbm, wq_hbm, wk_hbm, wv_hbm, wo_hbm, wg_hbm, wu_hbm, wd_hbm,
                 dx_out, dwk_out, dwv_out, xo, yo, do, ho,
                 xg, yg, wall, wy, dd, hos, dhs, qs, ks, vs, dka, dva, sc, pb, ds, wqv, wkv, ktmp,
                 dxs, rsend, drecv, rrecv, kvp, kr1, kr2, kr3,
                 wsem, ring_s, sib_s, rsem, lsem, hsem, osem, d_s, d_r, r_s, r_r, k_s, k_r):
    S = z_
    n, chips, tok, pair, d_model, hd = S.n, S.chips, S.tok, S.pair, S.d, S.hd
    sub_rows = tok // SUBS
    scale = hd ** -0.5
    me = lax.axis_index("tp")
    c = lax.rem(me, 2)
    z = lax.div(me, 2)
    step_dir = 1 - 2 * c
    dev = lambda chip: lax.rem(chip + chips, chips) * 2 + c
    nxt, prv = dev(z + step_dir), dev(z - step_dir)
    sib = me + 1 - 2 * c
    a0, a1 = lax.rem(z, 2), lax.rem(lax.div(z, 2), 2)
    part1 = (z + 1 - 2 * a0) * 2 + c
    part2 = (z + 2 - 4 * a1) * 2 + c
    kvi = lax.div(me, n // S.kv)

    barrier = pltpu.get_barrier_semaphore()
    for peer in (sib, nxt, prv, part2):
        pl.semaphore_signal(barrier, inc=1, device_id={"tp": peer}, device_id_type=MESH)

    fm, ft = S.fm, S.ft
    wcopies = [
        pltpu.make_async_copy(wg_hbm.at[pl.ds(0, fm)], wall.at[pl.ds(0, fm)], wsem.at[0]),
        pltpu.make_async_copy(wu_hbm.at[pl.ds(0, fm)], wall.at[pl.ds(S.au, fm)], wsem.at[1]),
        pltpu.make_async_copy(wg_hbm.at[pl.ds(fm, ft)], wall.at[pl.ds(S.at, ft)], wsem.at[2]),
        pltpu.make_async_copy(wu_hbm.at[pl.ds(fm, ft)], wall.at[pl.ds(S.at + ft, ft)], wsem.at[3]),
        pltpu.make_async_copy(wd_hbm.at[pl.ds(0, fm)], wy.at[pl.ds(0, fm)], wsem.at[4]),
        pltpu.make_async_copy(wd_hbm.at[pl.ds(fm, ft)], wy.at[pl.ds(S.yt, ft)], wsem.at[5]),
        pltpu.make_async_copy(wo_hbm, wy.at[pl.ds(S.yo, hd)], wsem.at[6]),
    ]
    qcopy = pltpu.make_async_copy(wq_hbm, wqv, wsem.at[7])
    kcopy = pltpu.make_async_copy(wk_hbm, wkv.at[0], wsem.at[8])
    vcopy = pltpu.make_async_copy(wv_hbm, wkv.at[1], wsem.at[9])
    for cp in [qcopy, kcopy, vcopy] + wcopies:
        cp.start()

    gathered, owned = (xg, yg), (x_hbm, y_hbm)

    def rows(slot, ring, sub):
        return pl.ds(pl.multiple_of(slot * pair + ring * tok + sub * sub_rows, sub_rows), sub_rows)

    def ring_copy(st, slot, sub, src):
        return pltpu.make_async_remote_copy(
            src_ref=src, dst_ref=gathered[st].at[rows(slot + 1, c, sub)],
            send_sem=ring_s.at[st, slot, sub], recv_sem=rsem.at[st, slot + 1, c, sub],
            device_id={"tp": nxt}, device_id_type=MESH)

    def sib_copy(st, slot, sub, src):
        return pltpu.make_async_remote_copy(
            src_ref=src, dst_ref=gathered[st].at[rows(slot, c, sub)],
            send_sem=sib_s.at[st, slot, sub], recv_sem=rsem.at[st, slot, c, sub],
            device_id={"tp": sib}, device_id_type=MESH)

    def own_src(st, sub):
        return owned[st].at[pl.ds(sub * sub_rows, sub_rows)]

    def here(st, slot, sub):
        return gathered[st].at[rows(slot, c, sub)]

    def wait_block(st, slot, ring, sub):
        ref = gathered[st].at[rows(slot, ring, sub)]
        pltpu.make_async_remote_copy(
            src_ref=ref, dst_ref=ref, send_sem=ring_s.at[st, 0, sub], recv_sem=rsem.at[st, slot, ring, sub],
            device_id={"tp": sib}, device_id_type=MESH).wait_recv()

    def start_own(st):
        for sub in range(SUBS):
            ring_copy(st, 0, sub, own_src(st, sub)).start()
            sib_copy(st, 0, sub, own_src(st, sub)).start()

    def pump(st, slot, sub):
        wait_block(st, slot, c, sub)

        @pl.when(slot < chips - 1)
        def _():
            ring_copy(st, slot, sub, here(st, slot, sub)).start()
        sib_copy(st, slot, sub, here(st, slot, sub)).start()

    local = [pltpu.make_async_copy(owned[st], gathered[st].at[pl.ds(pl.multiple_of(c * tok, tok), tok)], lsem.at[st])
             for st in range(2)]
    for cp in local:
        cp.start()
    pl.semaphore_wait(barrier, 4)
    start_own(0)

    wall[S.at + 2 * ft:S.wa, :] = jnp.zeros((128 - 2 * ft, d_model), BF)
    wy[S.yt + ft:S.wy, :] = jnp.zeros((128 - ft, d_model), BF)
    dka[...] = jnp.zeros_like(dka)
    dva[...] = jnp.zeros_like(dva)
    qcopy.wait()
    kcopy.wait()
    vcopy.wait()
    span = 256

    @pl.loop(0, d_model // span)
    def _(i):
        r0 = pl.multiple_of(i * span, span)
        wall[S.aq:S.aq + hd, pl.ds(r0, span)] = wqv[pl.ds(r0, span), :].T
        for w in range(2):
            ktmp[...] = wkv[w, pl.ds(r0, span)].reshape(S.kv * span, hd).astype(F32)
            one = ktmp[pl.ds(kvi, span, stride=S.kv), :]
            off = S.ak + w * hd
            wall[off:off + hd, pl.ds(r0, span)] = one.T.astype(BF)
    for cp in wcopies:
        cp.wait()
    for cp in local:
        cp.wait()

    def block_of(slot, ring):
        chip = lax.rem(z + chips + jnp.where(ring == 0, -slot, slot), chips)
        return chip * 2 + ring

    def slot_rows(slot):
        return pl.ds(pl.multiple_of(slot * pair, pair), pair)

    cut = 1024

    def fwd_first(slot):
        out = dot_nt(xg[slot_rows(slot), :], wall[0:cut, :])
        dd[slot_rows(slot), 0:cut] = out.astype(BF)

    def fwd_second(slot):
        out = dot_nt(xg[slot_rows(slot), :], wall[cut:S.wa, :]).astype(BF)
        dd[slot_rows(slot), cut:S.wa] = out
        for ring in range(2):
            tgt = pl.ds(pl.multiple_of(block_of(slot, ring) * tok, tok), tok)
            part = out[ring * tok:(ring + 1) * tok]
            qs[tgt, :] = part[:, S.aq - cut:S.ak - cut]
            ks[tgt, :] = part[:, S.ak - cut:S.av - cut]
            vs[tgt, :] = part[:, S.av - cut:S.at - cut]

    @pl.loop(1, chips + 1)
    def _(it):
        @pl.when(it < chips)
        def _():
            pump(0, it, 0)
        for sub in range(SUBS):
            wait_block(0, it - 1, 1 - c, sub)
        fwd_first(it - 1)

        @pl.when(it < chips)
        def _():
            pump(0, it, 1)

        @pl.when(it == chips - 2)
        def _():
            start_own(1)
        fwd_second(it - 1)

    xcopy = pltpu.make_async_copy(xg, xo, osem.at[0])
    xcopy.start()

    def h_copy(slot):
        return pltpu.make_async_copy(hos.at[lax.rem(slot, 2)], ho.at[slot_rows(slot)], hsem.at[lax.rem(slot, 2)])

    lane = lax.broadcasted_iota(jnp.int32, (32, 128), 1)

    def mlp_mid(slot):
        buf = lax.rem(slot, 2)

        @pl.loop(0, pair // 32)
        def _(i):
            r = pl.ds(pl.multiple_of(slot * pair + i * 32, 32), 32)
            rl = pl.ds(pl.multiple_of(i * 32, 32), 32)

            def grads(a, u, dh):
                sg = jax.nn.sigmoid(a)
                act = a * sg
                return act * u, dh * u * sg * (1.0 + a * (1.0 - sg)), dh * act

            for j in range(0, fm, 128):
                h, da, du = grads(dd[r, j:j + 128].astype(F32), dd[r, S.au + j:S.au + j + 128].astype(F32), dhs[rl, j:j + 128])
                hos[buf, rl, j:j + 128] = h.astype(BF)
                dd[r, j:j + 128] = da.astype(BF)
                dd[r, S.au + j:S.au + j + 128] = du.astype(BF)
            both = dd[r, S.at:S.wa].astype(F32)
            h, da, du = grads(both, pltpu.roll(both, 128 - ft, 1), dhs[rl, S.yt:S.wy])
            hos[buf, rl, S.yt:S.wy] = h.astype(BF)
            rest = jnp.where(lane < ft, da, jnp.where(lane < 2 * ft, pltpu.roll(du, ft, 1), 0.0))
            dd[r, S.at:S.wa] = rest.astype(BF)

    kc = 256

    def attend(slot, ring, blk, chunks):
        rl = pl.ds(pl.multiple_of(ring * tok, tok), tok)
        qrow = pl.ds(pl.multiple_of(blk * tok, tok), tok)
        q = qs[qrow, :]
        dout = dhs[rl, S.yo:S.yt].astype(BF)
        run = None
        for ch in range(chunks):
            s = dot_nt(q, ks[ch * kc:(ch + 1) * kc, :]) * scale
            if ch >= chunks - 2:
                col = lax.broadcasted_iota(jnp.int32, (tok, kc), 1) + ch * kc
                row = lax.broadcasted_iota(jnp.int32, (tok, kc), 0) + blk * tok
                s = jnp.where(col <= row, s, -jnp.inf)
            sc[:, ch * kc:(ch + 1) * kc] = s
            top = jnp.maximum(s[:, 0:128], s[:, 128:256])
            run = top if run is None else jnp.maximum(run, top)
        m = jnp.max(run, axis=1, keepdims=True)
        tot = jnp.zeros((tok, 128), F32)
        for ch in range(chunks):
            p = jnp.exp(sc[:, ch * kc:(ch + 1) * kc] - m)
            sc[:, ch * kc:(ch + 1) * kc] = p
            tot = tot + p[:, 0:128] + p[:, 128:256]
        inv = 1.0 / jnp.sum(tot, axis=1, keepdims=True)
        for ch in range(chunks):
            p = sc[:, ch * kc:(ch + 1) * kc] * inv
            sc[:, ch * kc:(ch + 1) * kc] = p
            pb[:, ch * kc:(ch + 1) * kc] = p.astype(BF)
        length = chunks * kc
        o = dot_nn(pb[:, 0:length], vs[0:length, :]).astype(BF)
        hos[lax.rem(slot, 2), rl, S.yo:S.yt] = o
        delta = jnp.sum(dout.astype(F32) * o.astype(F32), axis=1, keepdims=True)
        for ch in range(chunks):
            dp = dot_nt(dout, vs[ch * kc:(ch + 1) * kc, :])
            ds[:, ch * kc:(ch + 1) * kc] = (sc[:, ch * kc:(ch + 1) * kc] * (dp - delta)).astype(BF)
        dq = dot_nn(ds[:, 0:length], ks[0:length, :]) * scale
        dd[pl.ds(pl.multiple_of(slot * pair + ring * tok, tok), tok), S.aq:S.ak] = dq.astype(BF)
        for ch in range(chunks):
            dka[ch * kc:(ch + 1) * kc, :] += dot_tn(ds[:, ch * kc:(ch + 1) * kc], q)
            dva[ch * kc:(ch + 1) * kc, :] += dot_tn(pb[:, ch * kc:(ch + 1) * kc], dout)

    @pl.loop(1, chips + 1)
    def _(it):
        slot = it - 1

        @pl.when(it < chips)
        def _():
            pump(1, it, 0)
        for sub in range(SUBS):
            wait_block(1, slot, 1 - c, sub)
        dhs[...] = dot_nt(yg[slot_rows(slot), :], wy[...])

        @pl.when(it < chips)
        def _():
            pump(1, it, 1)

        @pl.when(slot >= 2)
        def _():
            h_copy(slot - 2).wait()
        mlp_mid(slot)

        @pl.loop(0, 2)
        def _(ring):
            blk = block_of(slot, ring)
            group = lax.div(blk, 4)
            for v in range(n // 4):
                @pl.when(group == v)
                def _():
                    attend(slot, ring, blk, 2 * (v + 1))
        h_copy(slot).start()

    ycopy = pltpu.make_async_copy(yg, yo, osem.at[1])
    ycopy.start()

    @pl.loop(0, chips)
    def _(slot):
        for ring in range(2):
            src = pl.ds(pl.multiple_of(block_of(slot, ring) * tok, tok), tok)
            dst = pl.ds(pl.multiple_of(slot * pair + ring * tok, tok), tok)
            dd[dst, S.ak:S.av] = (dka[src, :] * scale).astype(BF)
            dd[dst, S.av:S.at] = dva[src, :].astype(BF)

    dcopy = pltpu.make_async_copy(dd, do, osem.at[2])
    dcopy.start()

    def slot_at(k):
        return lax.rem(k + 1, chips)

    def mine(ref, k):
        return ref.at[lax.rem(k, 2), pl.ds(pl.multiple_of(c * tok, tok), tok)]

    def d_copy(k):
        return pltpu.make_async_remote_copy(
            src_ref=dxs.at[lax.rem(k, 2), pl.ds(pl.multiple_of((1 - c) * tok, tok), tok)], dst_ref=drecv.at[k],
            send_sem=d_s.at[k], recv_sem=d_r.at[k], device_id={"tp": sib}, device_id_type=MESH)

    def r_copy(k, sub):
        cut_rows = pl.ds(sub * sub_rows, sub_rows)
        return pltpu.make_async_remote_copy(
            src_ref=rsend.at[lax.rem(k, 2), cut_rows], dst_ref=rrecv.at[k + 1, cut_rows],
            send_sem=r_s.at[k, sub], recv_sem=r_r.at[k + 1, sub], device_id={"tp": nxt}, device_id_type=MESH)

    def dx_part(k):
        slot = slot_at(k)
        buf = lax.rem(k, 2)
        lhs = dd[slot_rows(slot), :]
        for nb in range(0, d_model, 512):
            dxs[buf, :, nb:nb + 512] = dot_nn(lhs, wall[:, nb:nb + 512]).astype(BF)
        d_copy(k).start()

    def dx_pump(k, sub):
        cut_rows = pl.ds(sub * sub_rows, sub_rows)
        mine_rows = pl.ds(pl.multiple_of(c * tok + sub * sub_rows, sub_rows), sub_rows)

        @pl.when(k > 0)
        def _():
            rref = rrecv.at[k, cut_rows]
            pltpu.make_async_remote_copy(
                src_ref=rref, dst_ref=rref, send_sem=r_s.at[0, sub], recv_sem=r_r.at[k, sub],
                device_id={"tp": nxt}, device_id_type=MESH).wait_recv()

        @pl.when(jnp.logical_and(k >= 2, k < chips - 1))
        def _():
            r_copy(k - 2, sub).wait_send()
        base = dxs[lax.rem(k, 2), mine_rows, :].astype(F32) + drecv[k, cut_rows, :].astype(F32)

        @pl.when(k == 0)
        def _():
            rsend[0, cut_rows, :] = base.astype(BF)

        @pl.when(jnp.logical_and(k > 0, k < chips - 1))
        def _():
            rsend[lax.rem(k, 2), cut_rows, :] = (base + rrecv[k, cut_rows, :].astype(F32)).astype(BF)

        @pl.when(k == chips - 1)
        def _():
            dx_out[cut_rows, :] = (base + rrecv[k, cut_rows, :].astype(F32)).astype(BF)

        @pl.when(k < chips - 1)
        def _():
            r_copy(k, sub).start()

    k1 = pltpu.make_async_remote_copy(src_ref=kvp.at[1 - c], dst_ref=kr1, send_sem=k_s.at[0], recv_sem=k_r.at[0],
                                      device_id={"tp": sib}, device_id_type=MESH)
    k2 = pltpu.make_async_remote_copy(src_ref=kvp.at[c, 1 - a0], dst_ref=kr2, send_sem=k_s.at[1], recv_sem=k_r.at[1],
                                      device_id={"tp": part1}, device_id_type=MESH)
    k3 = pltpu.make_async_remote_copy(src_ref=kvp.at[c, a0, 1 - a1], dst_ref=kr3, send_sem=k_s.at[2], recv_sem=k_r.at[2],
                                      device_id={"tp": part2}, device_id_type=MESH)

    def kv_start():
        lhs = dd[:, S.ak:S.at]
        for e in range(n // S.kv):
            out = dot_tn(lhs, xg[:, e * kc:(e + 1) * kc])
            kvp[e % 2, (e // 2) % 2, e // 4] = out
        k1.start()

    def kv_second():
        k1.wait_recv()
        kvp[c] = kvp[c] + kr1[...]
        k2.start()

    def kv_third():
        k2.wait_recv()
        kvp[c, a0] = kvp[c, a0] + kr2[...]
        k3.start()

    def kv_last():
        k3.wait_recv()
        fin = kvp[c, a0, a1] + kr3[...]
        dwk_out[0] = fin[0:hd].T
        dwv_out[0] = fin[hd:2 * hd].T

    dx_part(0)

    @pl.loop(0, chips)
    def _(k):
        dref = drecv.at[k]
        pltpu.make_async_remote_copy(
            src_ref=dref, dst_ref=dref, send_sem=d_s.at[0], recv_sem=d_r.at[k],
            device_id={"tp": sib}, device_id_type=MESH).wait_recv()
        dx_pump(k, 0)

        @pl.when(jnp.logical_and(k >= 1, k < chips - 1))
        def _():
            d_copy(k - 1).wait_send()

        @pl.when(k < chips - 1)
        def _():
            dx_part(k + 1)
        dx_pump(k, 1)

        @pl.when(k == 0)
        def _():
            kv_start()

        @pl.when(k == 1)
        def _():
            kv_second()

        @pl.when(k == 4)
        def _():
            kv_third()

    kv_last()

    for cp in (k1, k2, k3):
        cp.wait_send()
    for sub in range(SUBS):
        for k in range(chips - 3, chips - 1):
            r_copy(k, sub).wait_send()
    for k in range(chips - 2, chips):
        d_copy(k).wait_send()

    @pl.loop(0, chips)
    def _(slot):
        for st in range(2):
            for sub in range(SUBS):
                @pl.when(slot < chips - 1)
                def _():
                    ring_copy(st, slot, sub, here(st, slot, sub)).wait_send()
                sib_copy(st, slot, sub, here(st, slot, sub)).wait_send()
    for slot in range(chips - 2, chips):
        h_copy(slot).wait()
    xcopy.wait()
    ycopy.wait()
    dcopy.wait()


def weights_kernel(z_, x_ref, y_ref, d_ref, h_ref, wg_out, wu_out, wd_out, wq_out, wo_out):
    S = z_
    fm, ft, hd = S.fm, S.ft, S.hd
    x, y = x_ref[...], y_ref[...]
    wg_out[0:fm, :] = dot_tn(d_ref[:, 0:fm], x)
    wu_out[0:fm, :] = dot_tn(d_ref[:, S.au:S.au + fm], x)
    wq_out[...] = dot_tn(d_ref[:, S.aq:S.ak], x).T
    rest = dot_tn(d_ref[:, S.at:S.wa], x)
    wg_out[fm:fm + ft, :] = rest[0:ft]
    wu_out[fm:fm + ft, :] = rest[ft:2 * ft]
    wd_out[0:fm, :] = dot_tn(h_ref[:, 0:fm], y)
    rest = dot_tn(h_ref[:, S.yo:S.wy], y)
    wo_out[...] = rest[0:hd]
    wd_out[fm:fm + ft, :] = rest[hd:hd + ft]


def solution(mesh):
    n_dev = mesh.shape["tp"]

    def local_step(x_loc, dy_loc, w_q, w_k, w_v, w_o, w_gate, w_up, w_down):
        tok, d_model = x_loc.shape
        ff, hd, kv = w_gate.shape[1], w_q.shape[2], w_k.shape[1]
        S = Sizes(n_dev, kv, tok, d_model, ff, hd)
        seq, chips, pair = S.seq, S.chips, S.pair
        any_spec = pl.BlockSpec(memory_space=pl.ANY)
        vm = pl.BlockSpec(memory_space=pltpu.VMEM)
        dma = pltpu.SemaphoreType.DMA
        reps = n_dev // kv
        dcut = d_model // reps
        outs = pl.pallas_call(
            functools.partial(fused_kernel, S),
            out_shape=(
                jax.ShapeDtypeStruct((tok, d_model), BF),
                jax.ShapeDtypeStruct((1, dcut, hd), F32),
                jax.ShapeDtypeStruct((1, dcut, hd), F32),
                jax.ShapeDtypeStruct((seq, d_model), BF),
                jax.ShapeDtypeStruct((seq, d_model), BF),
                jax.ShapeDtypeStruct((seq, S.wa), BF),
                jax.ShapeDtypeStruct((seq, S.wy), BF),
            ),
            in_specs=[any_spec] * 9,
            out_specs=(vm, vm, vm) + (any_spec,) * 4,
            scratch_shapes=[
                pltpu.VMEM((seq, d_model), BF), pltpu.VMEM((seq, d_model), BF),
                pltpu.VMEM((S.wa, d_model), BF), pltpu.VMEM((S.wy, d_model), BF),
                pltpu.VMEM((seq, S.wa), BF), pltpu.VMEM((2, pair, S.wy), BF), pltpu.VMEM((pair, S.wy), F32),
                pltpu.VMEM((seq, hd), BF), pltpu.VMEM((seq, hd), BF), pltpu.VMEM((seq, hd), BF),
                pltpu.VMEM((seq, hd), F32), pltpu.VMEM((seq, hd), F32),
                pltpu.VMEM((tok, seq), F32), pltpu.VMEM((tok, seq), BF), pltpu.VMEM((tok, seq), BF),
                pltpu.VMEM((d_model, hd), BF), pltpu.VMEM((2, d_model, kv, hd), BF), pltpu.VMEM((kv * 256, hd), F32),
                pltpu.VMEM((2, pair, d_model), BF), pltpu.VMEM((2, tok, d_model), BF),
                pltpu.VMEM((chips, tok, d_model), BF), pltpu.VMEM((chips, tok, d_model), BF),
                pltpu.VMEM((2, 2, reps // 4, 2 * hd, dcut), F32), pltpu.VMEM((2, reps // 4, 2 * hd, dcut), F32),
                pltpu.VMEM((reps // 4, 2 * hd, dcut), F32), pltpu.VMEM((2 * hd, dcut), F32),
                dma((10,)), dma((2, chips, SUBS)), dma((2, chips, SUBS)), dma((2, chips, 2, SUBS)), dma((2,)), dma((2,)),
                dma((3,)), dma((chips,)), dma((chips,)), dma((chips, SUBS)), dma((chips, SUBS)), dma((3,)), dma((3,)),
            ],
            compiler_params=pltpu.CompilerParams(collective_id=0, has_side_effects=True, vmem_limit_bytes=67043328),
            name="fused",
        )(x_loc, dy_loc, w_q[:, 0, :], w_k, w_v, w_o[0], w_gate.T, w_up.T, w_down)
        dx, dwk, dwv, xo, yo, do, ho = outs
        nb = 256
        col = lambda i: (0, i)
        fixed = lambda i: (0, 0)
        wg, wu, wd, wq, wo = pl.pallas_call(
            functools.partial(weights_kernel, S),
            grid=(d_model // nb,),
            in_specs=[pl.BlockSpec((seq, nb), col), pl.BlockSpec((seq, nb), col),
                      pl.BlockSpec((seq, S.wa), fixed), pl.BlockSpec((seq, S.wy), fixed)],
            out_specs=[pl.BlockSpec((ff, nb), col), pl.BlockSpec((ff, nb), col), pl.BlockSpec((ff, nb), col),
                       pl.BlockSpec((nb, hd), lambda i: (i, 0)), pl.BlockSpec((hd, nb), col)],
            out_shape=(jax.ShapeDtypeStruct((ff, d_model), F32), jax.ShapeDtypeStruct((ff, d_model), F32),
                       jax.ShapeDtypeStruct((ff, d_model), F32), jax.ShapeDtypeStruct((d_model, hd), F32),
                       jax.ShapeDtypeStruct((hd, d_model), F32)),
            compiler_params=pltpu.CompilerParams(vmem_limit_bytes=60 << 20),
            name="weights",
        )(xo, yo, do, ho)
        return (dx, wq.reshape(d_model, 1, hd), dwk, dwv, wo[None], wg.T, wu.T, wd)

    token_spec = P(("dp", "tp"), None)
    in_specs = (token_spec, token_spec, P(None, "tp", None), P(None, None, None), P(None, None, None),
                P("tp", None, None), P(None, "tp"), P(None, "tp"), P("tp", None))
    out_specs = (token_spec, P("dp", "tp", None), P(("dp", "tp"), None, None), P(("dp", "tp"), None, None),
                 P(("dp", "tp"), None, None), P("dp", "tp"), P("dp", "tp"), P(("dp", "tp"), None))
    return jax.shard_map(local_step, mesh=mesh, in_specs=in_specs, out_specs=out_specs, check_vma=False)
```

profile of v0, /device:TPU:21, one launch (start us, length us, event | category | flops | bytes accessed | tf_op | source)
XLA Modules:
  0.0 199.6 jit_solution(4118294556367140636)
XLA Ops:
  0.6 168.5 %fused.1 = (bf16[128,2048]{1,0:T(8,128)(2,1)}, f32[1,256,128]{2,1,0:T(8,128)}, f32[1,256,128]{2,1,0:T(8,128)}, bf16[2048,2048]{1,0:T(8,128)(2,1)}, bf16[2048,204...) custom-call(bf16[128,2048]{1,0:T(8,128)(2,1)} %x_hbm.1, bf16[128,2048]{1,0:T(8,128)(2,1)} %y_hbm.1, ...), custom_call_target="tpu_custom_call" | custom-call | tf_op jit(solution)/shard_map/fused/pallas_call | solution.py:487
  169.2 0.0 copy-start
  169.2 0.0 copy-start.2
  169.2 0.0 copy-start.1
  169.2 28.3 %weights.1 = (f32[688,2048]{1,0:T(8,128)}, f32[688,2048]{1,0:T(8,128)}, f32[688,2048]{1,0:T(8,128)}, f32[2048,128]{1,0:T(8,128)}, f32[128,2048]{1,0:T(8,128)}) custom-call(bf16[2048,2048]{1,0:T(8,128)(2,1)} %get-tuple-element.21.x_ref, bf16[2048,2048]{1,0:T(8,128)(2,1)} %get-tuple-element.22.y_ref, bf16[2048,1792]{1,0:T(8,128)(2,1)} %get-tuple-element.23.d_ref, ...), custom_call_target="tpu_custom_call" | custom-call | tf_op jit(solution)/shard_map/weights/pallas_call | solution.py:522
  197.5 0.0 copy-done
  197.5 0.8 copy.21
  198.3 0.0 copy-done.2
  198.3 0.7 copy.22
  199.0 0.0 copy-done.1
  199.0 0.7 copy.23
Async XLA Ops:
  169.2 28.4 %copy-start = (bf16[128,2048]{1,0:T(8,128)(2,1)S(1)}, bf16[128,2048]{1,0:T(8,128)(2,1)}, u32[]{:S(2)}) copy-start(bf16[128,2048]{1,0:T(8,128)(2,1)} %get-tuple-element.48) | copy-start | bytes 1572868
  169.2 29.1 %copy-start.2 = (f32[1,256,128]{2,1,0:T(8,128)S(1)}, f32[1,256,128]{2,1,0:T(8,128)}, u32[]{:S(2)}) copy-start(f32[1,256,128]{2,1,0:T(8,128)} %get-tuple-element.50) | copy-start | bytes 393220
  169.2 29.8 %copy-start.1 = (f32[1,256,128]{2,1,0:T(8,128)S(1)}, f32[1,256,128]{2,1,0:T(8,128)}, u32[]{:S(2)}) copy-start(f32[1,256,128]{2,1,0:T(8,128)} %get-tuple-element.51) | copy-start | bytes 393220
where the time goes:
time: 200 us
  Pallas kernels  197 us (98%)
  local copies, waits for them, and re-layouts  2.12 us (1%)
    pallas_call x1, Pallas kernels, local_step(): pl.pallas_call(functools.partial(fused_kernel, S), out_shape=(jax.ShapeDt...  169 us
    pallas_call x1, Pallas kernels, local_step(): pl.pallas_call(functools.partial(weights_kernel, S), grid=(d_model // nb,...  28.3 us

commit v1 on v0

v1 whole, which is shorter than its diff:
```python
import functools

import jax
import jax.numpy as jnp
from jax import lax
from jax.experimental import pallas as pl
from jax.experimental.pallas import tpu as pltpu
from jax.sharding import PartitionSpec as P

MESH = pl.DeviceIdType.MESH
BF = jnp.bfloat16
F32 = jnp.float32
SUBS = 2
KV_PARTS, KV_LAG = 8, 2


def dot_nt(a, b):
    return lax.dot_general(a, b, (((1,), (1,)), ((), ())), preferred_element_type=F32)


def dot_tn(a, b):
    return lax.dot_general(a, b, (((0,), (0,)), ((), ())), preferred_element_type=F32)


def dot_nn(a, b):
    return jnp.dot(a, b, preferred_element_type=F32)


class Sizes:
    def __init__(self, n_dev, kv_count, tok, d_model, ff, hd):
        self.n, self.kv, self.tok, self.d, self.ff, self.hd = n_dev, kv_count, tok, d_model, ff, hd
        self.chips = n_dev // 2
        self.seq = n_dev * tok
        self.fm = (ff // 128) * 128
        self.ft = ff - self.fm
        assert 0 < 2 * self.ft <= 128 and self.ft % 16 == 0 and hd == 128 and tok == 128
        self.au, self.aq, self.at = self.fm, 2 * self.fm, 2 * self.fm + hd
        self.ak = self.at + 128
        self.av, self.wa = self.ak + hd, self.ak + 2 * hd
        self.yt, self.yo = self.fm, self.fm + 128
        self.wy = self.yo + hd
        self.pair = 2 * tok


def fused_kernel(z_, x_hbm, y_hbm, wq_hbm, wk_hbm, wv_hbm, wo_hbm, wg_hbm, wu_hbm, wd_hbm,
                 dx_own, dx_send, dwk_out, dwv_out, wg_out, wu_out, wq_out, wd_out, wo_out,
                 xg, yg, wall, wy, dd, hh, dhs, dob, qs, ks, vs, pb, ds, wqv, wkv, ktmp,
                 dxs, rsend, drecv, rrecv, kvd, kvl, kvr, kvf, kvg, stage,
                 wsem, ring_s, sib_s, rsem, lsem, gsem, d_s, d_r, r_s, r_r, k_s, k_r, line_s, line_r):
    S = z_
    n, chips, tok, pair, d_model, hd = S.n, S.chips, S.tok, S.pair, S.d, S.hd
    sub_rows = tok // SUBS
    scale = hd ** -0.5
    me = lax.axis_index("tp")
    c = lax.rem(me, 2)
    z = lax.div(me, 2)
    step_dir = 1 - 2 * c
    dev = lambda chip: lax.rem(chip + chips, chips) * 2 + c
    nxt, prv = dev(z + step_dir), dev(z - step_dir)
    sib = me + 1 - 2 * c
    kvi = lax.div(me, n // S.kv)

    barrier = pltpu.get_barrier_semaphore()
    for peer in (sib, nxt, prv):
        pl.semaphore_signal(barrier, inc=1, device_id={"tp": peer}, device_id_type=MESH)

    fm, ft = S.fm, S.ft
    wcopies = [
        pltpu.make_async_copy(wg_hbm.at[pl.ds(0, fm)], wall.at[pl.ds(0, fm)], wsem.at[0]),
        pltpu.make_async_copy(wu_hbm.at[pl.ds(0, fm)], wall.at[pl.ds(S.au, fm)], wsem.at[1]),
        pltpu.make_async_copy(wg_hbm.at[pl.ds(fm, ft)], wall.at[pl.ds(S.at, ft)], wsem.at[2]),
        pltpu.make_async_copy(wu_hbm.at[pl.ds(fm, ft)], wall.at[pl.ds(S.at + ft, ft)], wsem.at[3]),
        pltpu.make_async_copy(wd_hbm.at[pl.ds(0, fm)], wy.at[pl.ds(0, fm)], wsem.at[4]),
        pltpu.make_async_copy(wd_hbm.at[pl.ds(fm, ft)], wy.at[pl.ds(S.yt, ft)], wsem.at[5]),
        pltpu.make_async_copy(wo_hbm, wy.at[pl.ds(S.yo, hd)], wsem.at[6]),
    ]
    qcopy = pltpu.make_async_copy(wq_hbm, wqv, wsem.at[7])
    kcopy = pltpu.make_async_copy(wk_hbm, wkv.at[0], wsem.at[8])
    vcopy = pltpu.make_async_copy(wv_hbm, wkv.at[1], wsem.at[9])
    gathered, owned = (xg, yg), (x_hbm, y_hbm)
    local = [pltpu.make_async_copy(owned[st], gathered[st].at[pl.ds(pl.multiple_of(c * tok, tok), tok)], lsem.at[st])
             for st in range(2)]
    for cp in local + [qcopy, kcopy, vcopy]:
        cp.start()

    def rows(slot, ring, sub):
        return pl.ds(pl.multiple_of(slot * pair + ring * tok + sub * sub_rows, sub_rows), sub_rows)

    def ring_copy(st, slot, sub, src):
        return pltpu.make_async_remote_copy(
            src_ref=src, dst_ref=gathered[st].at[rows(slot + 1, c, sub)],
            send_sem=ring_s.at[st, slot, sub], recv_sem=rsem.at[st, slot + 1, c, sub],
            device_id={"tp": nxt}, device_id_type=MESH)

    def sib_copy(st, slot, sub, src):
        return pltpu.make_async_remote_copy(
            src_ref=src, dst_ref=gathered[st].at[rows(slot, c, sub)],
            send_sem=sib_s.at[st, slot, sub], recv_sem=rsem.at[st, slot, c, sub],
            device_id={"tp": sib}, device_id_type=MESH)

    def here(st, slot, sub):
        return gathered[st].at[rows(slot, c, sub)]

    def wait_block(st, slot, ring, sub):
        ref = gathered[st].at[rows(slot, ring, sub)]
        pltpu.make_async_remote_copy(
            src_ref=ref, dst_ref=ref, send_sem=ring_s.at[st, 0, sub], recv_sem=rsem.at[st, slot, ring, sub],
            device_id={"tp": sib}, device_id_type=MESH).wait_recv()

    def start_ring(st):
        for sub in range(SUBS):
            ring_copy(st, 0, sub, here(st, 0, sub)).start()

    def start_sib(st):
        for sub in range(SUBS):
            sib_copy(st, 0, sub, here(st, 0, sub)).start()

    def pump(st, slot, sub):
        wait_block(st, slot, c, sub)

        @pl.when(slot < chips - 1)
        def _():
            ring_copy(st, slot, sub, here(st, slot, sub)).start()
        sib_copy(st, slot, sub, here(st, slot, sub)).start()

    pl.semaphore_wait(barrier, 3)
    local[0].wait()
    start_ring(0)
    local[1].wait()
    for st in range(2):
        start_sib(st)
    for cp in wcopies:
        cp.start()

    wall[S.at + 2 * ft:S.ak, :] = jnp.zeros((128 - 2 * ft, d_model), BF)
    wy[S.yt + ft:S.yo, :] = jnp.zeros((128 - ft, d_model), BF)
    for i in (1, 2):
        stage[i] = jnp.zeros(stage.shape[1:], F32)
    rrecv[0] = jnp.zeros(rrecv.shape[1:], BF)
    qcopy.wait()
    kcopy.wait()
    vcopy.wait()
    span = 256

    @pl.loop(0, d_model // span)
    def _(i):
        r0 = pl.multiple_of(i * span, span)
        wall[S.aq:S.aq + hd, pl.ds(r0, span)] = wqv[pl.ds(r0, span), :].T
        for w in range(2):
            ktmp[...] = wkv[w, pl.ds(r0, span)].reshape(S.kv * span, hd).astype(F32)
            one = ktmp[pl.ds(kvi, span, stride=S.kv), :]
            off = S.ak + w * hd
            wall[off:off + hd, pl.ds(r0, span)] = one.T.astype(BF)
    pump(0, 1, 0)
    for cp in wcopies:
        cp.wait()

    def block_of(slot, ring):
        chip = lax.rem(z + chips + jnp.where(ring == 0, -slot, slot), chips)
        return chip * 2 + ring

    def slot_rows(slot):
        return pl.ds(pl.multiple_of(slot * pair, pair), pair)

    cut = 1024

    def fwd_first(slot):
        out = dot_nt(xg[slot_rows(slot), :], wall[0:cut, :])
        dd[slot_rows(slot), 0:cut] = out.astype(BF)

    def fwd_second(slot):
        out = dot_nt(xg[slot_rows(slot), :], wall[cut:S.wa, :]).astype(BF)
        dd[slot_rows(slot), cut:S.wa] = out
        for ring in range(2):
            tgt = pl.ds(pl.multiple_of(block_of(slot, ring) * tok, tok), tok)
            part = out[ring * tok:(ring + 1) * tok]
            qs[tgt, :] = part[:, S.aq - cut:S.at - cut]
            ks[tgt, :] = part[:, S.ak - cut:S.av - cut]
            vs[tgt, :] = part[:, S.av - cut:S.wa - cut]

    lane = lax.broadcasted_iota(jnp.int32, (32, 128), 1)

    def mlp_mid(slot):
        @pl.loop(0, pair // 32)
        def _(i):
            r = pl.ds(pl.multiple_of(slot * pair + i * 32, 32), 32)
            rl = pl.ds(pl.multiple_of(i * 32, 32), 32)

            def grads(a, u, dh):
                sg = jax.nn.sigmoid(a)
                act = a * sg
                return act * u, dh * u * sg * (1.0 + a * (1.0 - sg)), dh * act

            for j in range(0, fm, 128):
                h, da, du = grads(dd[r, j:j + 128].astype(F32), dd[r, S.au + j:S.au + j + 128].astype(F32), dhs[rl, j:j + 128])
                hh[r, j:j + 128] = h.astype(BF)
                dd[r, j:j + 128] = da.astype(BF)
                dd[r, S.au + j:S.au + j + 128] = du.astype(BF)
            both = dd[r, S.at:S.ak].astype(F32)
            h, da, du = grads(both, pltpu.roll(both, 128 - ft, 1), dhs[rl, fm:fm + 128])
            hh[r, S.yt:S.yo] = h.astype(BF)
            rest = jnp.where(lane < ft, da, jnp.where(lane < 2 * ft, pltpu.roll(du, ft, 1), 0.0))
            dd[r, S.at:S.ak] = rest.astype(BF)

    def y_out(slot, ring):
        part = pl.ds(pl.multiple_of(slot * pair + ring * tok, tok), tok)
        dob[...] = dot_nt(yg[part, :], wy[S.yo:S.wy, :]).astype(BF)

    def y_first(slot):
        dhs[...] = dot_nt(yg[slot_rows(slot), :], wy[0:S.yo, :])

    for sub in range(SUBS):
        wait_block(1, 0, 1 - c, sub)
    y_first(0)

    @pl.loop(0, chips)
    def _(slot):
        for sub in range(SUBS):
            wait_block(0, slot, 1 - c, sub)
        fwd_first(slot)

        @pl.when(slot < chips - 1)
        def _():
            pump(0, slot + 1, 1)

        @pl.when(slot == chips - 3)
        def _():
            start_ring(1)

        @pl.when(slot == chips - 1)
        def _():
            pump(1, 1, 0)
        fwd_second(slot)

        @pl.when(slot == 0)
        def _():
            mlp_mid(0)

        @pl.when(slot < chips - 2)
        def _():
            pump(0, slot + 2, 0)

    kc = 256
    sc, dka, dva = stage.at[0], stage.at[1], stage.at[2]

    def attend(slot, ring, blk, chunks):
        qrow = pl.ds(pl.multiple_of(blk * tok, tok), tok)
        q = qs[qrow, :]
        dout = dob[...]
        srow = pl.ds(pl.multiple_of(slot * pair + ring * tok, tok), tok)
        run = None
        for ch in range(chunks):
            s = dot_nt(q, ks[ch * kc:(ch + 1) * kc, :]) * scale
            if ch >= chunks - 2:
                col = lax.broadcasted_iota(jnp.int32, (tok, kc), 1) + ch * kc
                row = lax.broadcasted_iota(jnp.int32, (tok, kc), 0) + blk * tok
                s = jnp.where(col <= row, s, -jnp.inf)
            sc[:, ch * kc:(ch + 1) * kc] = s
            top = jnp.maximum(s[:, 0:128], s[:, 128:256])
            run = top if run is None else jnp.maximum(run, top)
        m = jnp.max(run, axis=1, keepdims=True)
        tot = jnp.zeros((tok, 128), F32)
        for ch in range(chunks):
            p = jnp.exp(sc[:, ch * kc:(ch + 1) * kc] - m)
            sc[:, ch * kc:(ch + 1) * kc] = p
            tot = tot + p[:, 0:128] + p[:, 128:256]
        inv = 1.0 / jnp.sum(tot, axis=1, keepdims=True)
        for ch in range(chunks):
            p = sc[:, ch * kc:(ch + 1) * kc] * inv
            sc[:, ch * kc:(ch + 1) * kc] = p
            pb[:, ch * kc:(ch + 1) * kc] = p.astype(BF)
        length = chunks * kc
        o = dot_nn(pb[:, 0:length], vs[0:length, :]).astype(BF)
        hh[srow, S.yo:S.wy] = o
        delta = jnp.sum(dout.astype(F32) * o.astype(F32), axis=1, keepdims=True)
        for ch in range(chunks):
            dp = dot_nt(dout, vs[ch * kc:(ch + 1) * kc, :])
            ds[:, ch * kc:(ch + 1) * kc] = (sc[:, ch * kc:(ch + 1) * kc] * (dp - delta)).astype(BF)
        dq = dot_nn(ds[:, 0:length], ks[0:length, :]) * scale
        dd[srow, S.aq:S.at] = dq.astype(BF)
        for ch in range(chunks):
            for acc, lhs, rhs in ((dka, ds, q), (dva, pb, dout)):
                acc[:, ch * kc:(ch + 1) * kc] += dot_tn(rhs, lhs[:, ch * kc:(ch + 1) * kc])

    def attend_ring(slot, ring):
        blk = block_of(slot, ring)
        group = lax.div(blk, 4)
        for v in range(n // 4):
            @pl.when(group == v)
            def _():
                attend(slot, ring, blk, 2 * (v + 1))

    first_core = c == 0
    kv_in = pltpu.make_async_remote_copy(src_ref=ks, dst_ref=kvd, send_sem=k_s.at[0], recv_sem=k_r.at[0],
                                         device_id={"tp": sib}, device_id_type=MESH)

    def kv_own():
        for slot in range(chips):
            for ring in range(2):
                at = pl.multiple_of(block_of(slot, ring) * tok, tok)
                dst = slice(slot * pair + ring * tok, slot * pair + (ring + 1) * tok)
                dk = (dka[:, pl.ds(at, tok)] * scale).astype(BF).T
                dv = dva[:, pl.ds(at, tok)].astype(BF).T
                dd[dst, S.ak:S.av] = dk
                dd[dst, S.av:S.wa] = dv
                qs[pl.ds(at, tok), :] = jnp.where(first_core, dk, dv)
                ks[pl.ds(at, tok), :] = jnp.where(first_core, dv, dk)
        kv_in.start()

    def d_copy(k):
        return pltpu.make_async_remote_copy(
            src_ref=dxs.at[lax.rem(k, 2), pl.ds(pl.multiple_of((1 - c) * tok, tok), tok)], dst_ref=drecv.at[k],
            send_sem=d_s.at[k], recv_sem=d_r.at[k], device_id={"tp": sib}, device_id_type=MESH)

    def dx_part(k):
        buf = lax.rem(k, 2)
        lhs = dd[slot_rows(lax.rem(k + 1, chips)), :]
        for nb in range(0, d_model, 512):
            dxs[buf, :, nb:nb + 512] = dot_nn(lhs, wall[:, nb:nb + 512]).astype(BF)
        d_copy(k).start()

    @pl.loop(0, chips)
    def _(slot):
        y_out(slot, c)
        attend_ring(slot, c)

        @pl.when(jnp.logical_and(slot > 0, slot < chips - 1))
        def _():
            pump(1, slot + 1, 0)

        @pl.when(slot > 0)
        def _():
            for sub in range(SUBS):
                wait_block(1, slot, 1 - c, sub)
        y_out(slot, 1 - c)
        attend_ring(slot, 1 - c)

        @pl.when(slot == chips - 1)
        def _():
            kv_own()
            dx_part(jnp.int32(0))

        @pl.when(slot > 0)
        def _():
            y_first(slot)
            mlp_mid(slot)

        @pl.when(slot < chips - 1)
        def _():
            pump(1, slot + 1, 1)

    place = lax.rem(z, n // S.kv // 2)
    last_place = n // S.kv // 2 - 1
    kv_out = pltpu.make_async_remote_copy(src_ref=kvf, dst_ref=kvg, send_sem=k_s.at[1], recv_sem=k_r.at[1],
                                          device_id={"tp": sib}, device_id_type=MESH)
    parts, lag = KV_PARTS, KV_LAG
    part_rows = S.seq // parts

    def kv_part(i):
        return pl.ds(pl.multiple_of(i * part_rows, part_rows), part_rows)

    def line_copy(way, i):
        src, dst = ((ks, kvl), (vs, kvr))[way]
        to = dev(z + 1) if way == 0 else dev(z - 1)
        return pltpu.make_async_remote_copy(
            src_ref=src.at[kv_part(i)], dst_ref=dst.at[kv_part(i)], send_sem=line_s.at[way, i], recv_sem=line_r.at[way, i],
            device_id={"tp": to}, device_id_type=MESH)

    @pl.when(place == 0)
    def _():
        kvl[...] = jnp.zeros_like(kvl)

    @pl.when(place == last_place)
    def _():
        kvr[...] = jnp.zeros_like(kvr)

    def kv_begin():
        kv_in.wait()
        qs[...] = (qs[...].astype(F32) + kvd[...].astype(F32)).astype(BF)

    def kv_point(p):
        for way in range(2):
            at = place if way == 0 else last_place - place
            i = p - lag * at
            buf, got = ((ks, kvl), (vs, kvr))[way]

            @pl.when(jnp.logical_and(jnp.logical_and(i >= 0, i < parts), at < last_place))
            def _():
                @pl.when(at > 0)
                def _():
                    line_copy(way, i).wait_recv()
                buf[kv_part(i), :] = (qs[kv_part(i), :].astype(F32) + got[kv_part(i), :].astype(F32)).astype(BF)
                line_copy(way, i).start()

    def kv_sum():
        for way in range(2):
            at = place if way == 0 else last_place - place

            @pl.when(at == last_place)
            def _():
                for i in range(parts):
                    line_copy(way, i).wait_recv()
        kvf[...] = (qs[...].astype(F32) + kvl[...].astype(F32) + kvr[...].astype(F32)).astype(BF)
        kv_out.start()

    def kv_last():
        kv_out.wait()

        @pl.loop(0, chips)
        def _(slot):
            for ring in range(2):
                src = pl.ds(pl.multiple_of(block_of(slot, ring) * tok, tok), tok)
                dst = pl.ds(pl.multiple_of(slot * pair + ring * tok, tok), tok)
                dd[dst, S.ak:S.av] = jnp.where(first_core, kvf[src, :], kvg[src, :])
                dd[dst, S.av:S.wa] = jnp.where(first_core, kvg[src, :], kvf[src, :])
        own = pl.multiple_of(lax.rem(me, n // S.kv) * dwk_out.shape[1], 128)
        out = dot_tn(xg[:, pl.ds(own, dwk_out.shape[1])], dd[:, S.ak:S.wa])
        dwk_out[0] = out[:, 0:hd]
        dwv_out[0] = out[:, hd:2 * hd]

    def r_copy(k, sub):
        cut_rows = pl.ds(sub * sub_rows, sub_rows)
        return pltpu.make_async_remote_copy(
            src_ref=rsend.at[lax.rem(k, 2), cut_rows], dst_ref=rrecv.at[k + 1, cut_rows],
            send_sem=r_s.at[k, sub], recv_sem=r_r.at[k + 1, sub], device_id={"tp": nxt}, device_id_type=MESH)

    def d_wait(k):
        dref = drecv.at[k]
        pltpu.make_async_remote_copy(
            src_ref=dref, dst_ref=dref, send_sem=d_s.at[0], recv_sem=d_r.at[k],
            device_id={"tp": sib}, device_id_type=MESH).wait_recv()

    def dx_pump(k, sub):
        @pl.when(k > 0)
        def _():
            rref = rrecv.at[k, pl.ds(sub * sub_rows, sub_rows)]
            pltpu.make_async_remote_copy(
                src_ref=rref, dst_ref=rref, send_sem=r_s.at[0, sub], recv_sem=r_r.at[k, sub],
                device_id={"tp": nxt}, device_id_type=MESH).wait_recv()

        @pl.when(k >= 2)
        def _():
            r_copy(k - 2, sub).wait_send()
        buf = lax.rem(k, 2)
        for g in range(0, sub_rows, 16):
            at = pl.ds(sub * sub_rows + g, 16)
            mine = dxs[buf, pl.ds(pl.multiple_of(c * tok + sub * sub_rows + g, 16), 16), :].astype(F32)
            rsend[buf, at, :] = (mine + drecv[k, at, :].astype(F32) + rrecv[k, at, :].astype(F32)).astype(BF)

        @pl.when(k < chips - 2)
        def _():
            r_copy(k, sub).start()

    whole = fm // 128
    kinds = (
        (0, whole, ((wg_out, None, 0, 128),)), (whole, 2 * whole, ((wu_out, None, 0, 128),)),
        (2 * whole, 2 * whole + 1, ((wq_out, 0, 0, 128),)),
        (2 * whole + 1, 2 * whole + 2, ((wg_out, fm, 0, ft), (wu_out, fm, ft, ft))),
        (2 * whole + 2, 3 * whole + 2, ((wd_out, None, 0, 128),)), (3 * whole + 2, 3 * whole + 3, ((wd_out, fm, 0, ft),)),
        (3 * whole + 3, 3 * whole + 4, ((wo_out, 0, 0, 128),)),
    )
    x_units, units = 2 * whole + 2, 3 * whole + 4
    slots = stage.shape[0]

    def g_do(u, act):
        for lo, hi, pieces in kinds:
            @pl.when(jnp.logical_and(u >= lo, u < hi))
            def _():
                for i, (ref, dst, src, size) in enumerate(pieces):
                    row = pl.multiple_of((u - lo) * 128, 128) if dst is None else dst
                    slot = lax.rem(u, slots)
                    act(pltpu.make_async_copy(stage.at[slot, pl.ds(src, size)], ref.at[pl.ds(row, size)], gsem.at[slot, i]))

    def dw_unit(u):
        @pl.when(jnp.logical_and(u >= slots, u < units))
        def _():
            g_do(u - slots, lambda cp: cp.wait())
        slot = lax.rem(u, slots)
        for lhs, rhs, lo, hi in ((dd, xg, 0, x_units), (hh, yg, x_units, units)):
            @pl.when(jnp.logical_and(u >= lo, u < hi))
            def _():
                at = pl.ds(pl.multiple_of((u - lo) * 128, 128), 128)
                for nb in range(0, d_model, kc):
                    stage[slot, :, nb:nb + kc] = dot_tn(lhs[:, at], rhs[:, nb:nb + kc])
        g_do(u, lambda cp: cp.start())

    kv_begin()
    kv_point(0)

    @pl.loop(0, chips - 1)
    def _(k):
        d_wait(k)
        dx_pump(k, 0)
        kv_point(2 * k + 1)

        @pl.when(k >= 1)
        def _():
            d_copy(k - 1).wait_send()
        dx_part(k + 1)

        dw_unit(3 * k)
        dx_pump(k, 1)
        kv_point(2 * k + 2)

        @pl.when(k == chips - 2)
        def _():
            kv_sum()

        @pl.loop(0, 2)
        def _(i):
            dw_unit(3 * k + 1 + i)

    own_k = chips - 1
    dx_copy = pltpu.make_async_copy(rsend.at[(own_k - 1) % 2], dx_send, lsem.at[0])
    dx_copy.start()
    d_wait(own_k)
    buf = own_k % 2
    for g in range(0, tok, 16):
        mine = dxs[buf, pl.ds(pl.multiple_of(c * tok + g, 16), 16), :].astype(F32)
        dx_own[g:g + 16, :] = mine + drecv[own_k, g:g + 16, :].astype(F32)
    dx_copy.wait()
    kv_last()

    for way in range(2):
        at = place if way == 0 else last_place - place

        @pl.when(at < last_place)
        def _():
            for i in range(parts):
                line_copy(way, i).wait_send()
    for sub in range(SUBS):
        r_copy(chips - 3, sub).wait_send()
    for k in range(chips - 2, chips):
        d_copy(k).wait_send()

    @pl.loop(0, chips)
    def _(slot):
        for st in range(2):
            for sub in range(SUBS):
                @pl.when(slot < chips - 1)
                def _():
                    ring_copy(st, slot, sub, here(st, slot, sub)).wait_send()
                sib_copy(st, slot, sub, here(st, slot, sub)).wait_send()
    for u in range(units - slots, units):
        g_do(jnp.int32(u), lambda cp: cp.wait())


def finish_kernel(wg_hbm, wu_hbm, wd_hbm, wo_hbm, wq_hbm, dwk_hbm, dwv_hbm,
                  wg_out, wu_out, wd_out, wo_out, wq_out, dwk_out, dwv_out,
                  big, wov, wqv, wqt, kvb, isem, osem):
    half = big.shape[1] // 2
    moves = [(wq_hbm, wqv, None, None)]
    for w, (src, dst) in enumerate(((wg_hbm, wg_out), (wu_hbm, wu_out), (wd_hbm, wd_out))):
        for r in (0, half):
            moves.append((src.at[pl.ds(r, half)], big.at[w, pl.ds(r, half)], big.at[w, pl.ds(r, half)], dst.at[pl.ds(r, half)]))
    moves += [(wo_hbm, wov, wov, wo_out), (dwk_hbm, kvb.at[0], kvb.at[0], dwk_out), (dwv_hbm, kvb.at[1], kvb.at[1], dwv_out)]
    moves[0] = (wq_hbm, wqv, wqt, wq_out)
    into = [pltpu.make_async_copy(m[0], m[1], isem.at[i]) for i, m in enumerate(moves)]
    out = [pltpu.make_async_copy(m[2], m[3], osem.at[i]) for i, m in enumerate(moves)]
    for cp in into:
        cp.start()
    for i in range(len(moves)):
        into[i].wait()
        if i == 0:
            wqt[...] = wqv[...].T
        out[i].start()
    for cp in out:
        cp.wait()


def solution(mesh):
    n_dev = mesh.shape["tp"]

    def local_step(x_loc, dy_loc, w_q, w_k, w_v, w_o, w_gate, w_up, w_down):
        tok, d_model = x_loc.shape
        ff, hd, kv = w_gate.shape[1], w_q.shape[2], w_k.shape[1]
        S = Sizes(n_dev, kv, tok, d_model, ff, hd)
        seq, chips, pair = S.seq, S.chips, S.pair
        any_spec = pl.BlockSpec(memory_space=pl.ANY)
        vm = pl.BlockSpec(memory_space=pltpu.VMEM)
        dma = pltpu.SemaphoreType.DMA
        reps = n_dev // kv
        dcut = d_model // reps
        ff_out, hd_out = jax.ShapeDtypeStruct((ff, d_model), F32), jax.ShapeDtypeStruct((hd, d_model), F32)
        kv_out = jax.ShapeDtypeStruct((1, dcut, hd), F32)
        outs = pl.pallas_call(
            functools.partial(fused_kernel, S),
            out_shape=(
                jax.ShapeDtypeStruct((tok, d_model), F32),
                jax.ShapeDtypeStruct((tok, d_model), BF),
                kv_out, kv_out, ff_out, ff_out, hd_out, ff_out, hd_out,
            ),
            in_specs=[any_spec] * 9,
            out_specs=(vm, any_spec, vm, vm) + (any_spec,) * 5,
            scratch_shapes=[
                pltpu.VMEM((seq, d_model), BF), pltpu.VMEM((seq, d_model), BF),
                pltpu.VMEM((S.wa, d_model), BF), pltpu.VMEM((S.wy, d_model), BF),
                pltpu.VMEM((seq, S.wa), BF), pltpu.VMEM((seq, S.wy), BF), pltpu.VMEM((pair, S.fm + 128), F32), pltpu.VMEM((tok, hd), BF),
                pltpu.VMEM((seq, hd), BF), pltpu.VMEM((seq, hd), BF), pltpu.VMEM((seq, hd), BF),
                pltpu.VMEM((tok, seq), BF), pltpu.VMEM((tok, seq), BF),
                pltpu.VMEM((d_model, hd), BF), pltpu.VMEM((2, d_model, kv, hd), BF), pltpu.VMEM((kv * 256, hd), F32),
                pltpu.VMEM((2, pair, d_model), BF), pltpu.VMEM((2, tok, d_model), BF),
                pltpu.VMEM((chips, tok, d_model), BF), pltpu.VMEM((chips, tok, d_model), BF),
                pltpu.VMEM((seq, hd), BF), pltpu.VMEM((seq, hd), BF), pltpu.VMEM((seq, hd), BF),
                pltpu.VMEM((seq, hd), BF), pltpu.VMEM((seq, hd), BF),
                pltpu.VMEM((4, hd, d_model), F32),
                dma((10,)), dma((2, chips, SUBS)), dma((2, chips, SUBS)), dma((2, chips, 2, SUBS)), dma((2,)),
                dma((4, 2)), dma((chips,)), dma((chips,)), dma((chips, SUBS)), dma((chips, SUBS)), dma((2,)), dma((2,)),
                dma((2, KV_PARTS)), dma((2, KV_PARTS)),
            ],
            compiler_params=pltpu.CompilerParams(collective_id=0, has_side_effects=True, vmem_limit_bytes=67043328),
            name="fused",
        )(x_loc, dy_loc, w_q[:, 0, :], w_k, w_v, w_o[0], w_gate.T, w_up.T, w_down)
        dx_own, dx_send, dwk, dwv, wg, wu, wq, wd, wo = outs
        hop = [(i, (i + 2 - 4 * (i % 2)) % n_dev) for i in range(n_dev)]
        dx_last = lax.ppermute(dx_send, "tp", hop)
        wg, wu, wd, wo, wq, dwk, dwv = pl.pallas_call(
            finish_kernel,
            in_specs=[any_spec] * 7,
            out_specs=[any_spec] * 7,
            out_shape=(ff_out, ff_out, ff_out, hd_out, jax.ShapeDtypeStruct((d_model, hd), F32), kv_out, kv_out),
            scratch_shapes=[
                pltpu.VMEM((3, ff, d_model), F32), pltpu.VMEM((hd, d_model), F32), pltpu.VMEM((hd, d_model), F32),
                pltpu.VMEM((d_model, hd), F32), pltpu.VMEM((2, 1, dcut, hd), F32), dma((10,)), dma((10,)),
            ],
            cost_estimate=pl.CostEstimate(flops=10 ** 10, bytes_accessed=38 * 10 ** 6, transcendentals=0),
            compiler_params=pltpu.CompilerParams(vmem_limit_bytes=62 << 20),
            name="finish",
        )(wg, wu, wd, wo, wq, dwk, dwv)
        dx = (dx_own + dx_last.astype(F32)).astype(BF)
        return (dx, wq.reshape(d_model, 1, hd), dwk, dwv, wo[None], wg.T, wu.T, wd)

    token_spec = P(("dp", "tp"), None)
    in_specs = (token_spec, token_spec, P(None, "tp", None), P(None, None, None), P(None, None, None),
                P("tp", None, None), P(None, "tp"), P(None, "tp"), P("tp", None))
    out_specs = (token_spec, P("dp", "tp", None), P(("dp", "tp"), None, None), P(("dp", "tp"), None, None),
                 P(("dp", "tp"), None, None), P("dp", "tp"), P("dp", "tp"), P(("dp", "tp"), None))
    return jax.shard_map(local_step, mesh=mesh, in_specs=in_specs, out_specs=out_specs, check_vma=False)
```

time: 200 us -> 172 us (0.86)
  Pallas kernels: 197 us -> 168 us
  starting transfers between devices: 0 us -> 2.43 us
  local copies, waits for them, and re-layouts: 2.12 us -> 0.01 us
    pallas_call x1, Pallas kernels: 28.3 us -> 12.9 us  [local_step(): pl.pallas_call(finish_kernel, in_specs=[any_spec] * 7, out_specs=[any_spe...]
    pallas_call x1, Pallas kernels: 169 us -> 155 us  [local_step(): pl.pallas_call(functools.partial(fused_kernel, S), out_shape=(jax.ShapeDt...]
    ppermute x0 -> x1, starting transfers between devices: none -> 2.43 us  [local_step(): dx_last = lax.ppermute(dx_send, 'tp', hop)]
    unnamed x9 -> x2, local copies, waits for them, and re-layouts: 2.12 us -> 0.01 us
  transfers between devices with their start and end apart: 0 -> 1, of which waited for: 0 -> 0; matrix products, arithmetic and copies ran while one was open for 0% -> 0% of each run, Pallas kernels for 0% -> 8%
where the time goes in v1:
time: 172 us
  Pallas kernels  168 us (98%)
  starting transfers between devices  2.43 us (1%)
    pallas_call x1, Pallas kernels, local_step(): pl.pallas_call(functools.partial(fused_kernel, S), out_shape=(jax.ShapeDt...  155 us
    pallas_call x1, Pallas kernels, local_step(): pl.pallas_call(finish_kernel, in_specs=[any_spec] * 7, out_specs=[any_spe...  12.9 us
  transfers between devices with their start and end apart: 1, of which 0 were waited for; matrix products, arithmetic and copies ran while one was open for 0% of the time, Pallas kernels for 8%

profile of v1, /device:TPU:21, one launch (start us, length us, event | category | flops | bytes accessed | tf_op | source)
XLA Modules:
  0.0 171.6 jit_solution(1519571616689318203)
XLA Ops:
  0.6 154.6 %fused.1 = (f32[128,2048]{1,0:T(8,128)}, bf16[128,2048]{1,0:T(8,128)(2,1)}, f32[1,256,128]{2,1,0:T(8,128)}, f32[1,256,128]{2,1,0:T(8,128)}, f32[688,2048]{1,0:T(...) custom-call(bf16[128,2048]{1,0:T(8,128)(2,1)} %x_hbm.1, ...), custom_call_target="tpu_custom_call" | custom-call | tf_op jit(solution)/shard_map/fused/pallas_call | solution.py:586
  155.3 2.4 %collective-permute-start = (bf16[128,2048]{1,0:T(8,128)(2,1)}, bf16[128,2048]{1,0:T(8,128)(2,1)S(1)}, u32[]{:S(2)}, u32[]{:S(2)}) collective-permute-start(bf16[128,2048]{1,0:T(8,128)(2,1)} %get-tuple-element.25), channel_id=1, source_target_pairs={{0,2},{1,15},{2,4},{3,1},{4,6},{5,3},{6,8},{7,5},{8,10},{9,7},{10,... | collective-permute-start | bytes 1572872 | tf_op jit(solution)/shard_map/ppermute | solution.py:616
  157.7 0.0 copy-start
  157.7 12.9 %finish.1 = (f32[688,2048]{1,0:T(8,128)}, f32[688,2048]{1,0:T(8,128)}, f32[688,2048]{1,0:T(8,128)}, f32[128,2048]{1,0:T(8,128)}, f32[2048,128]{1,0:T(8,128)}, /*...) custom-call(f32[688,2048]{1,0:T(8,128)} %get-tuple-element.26.wg_hbm, f32[688,2048]{1,0:T(8,128)} %get-tuple-element.27.wu_hbm, ...), custom_call_target="tpu_custom_call" | custom-call | flops 10000000000 | bytes 38000000 | tf_op jit(solution)/shard_map/finish/pallas_call | solution.py:617
  170.6 0.0 collective-permute-done
  170.6 0.0 copy-done
  170.7 0.9 add_convert_fusion
Async XLA Ops:
  155.3 15.4 %collective-permute-start = (bf16[128,2048]{1,0:T(8,128)(2,1)}, bf16[128,2048]{1,0:T(8,128)(2,1)S(1)}, u32[]{:S(2)}, u32[]{:S(2)}) collective-permute-start(bf16[128,2048]{1,0:T(8,128)(2,1)} %get-tuple-element.25), channel_id=1, source_target_pairs={{0,2},{1,15},{2,4},{3,1},{4,6},{5,3},{6,8},{7,5},{8,10},{9,7},{10,... | collective-permute-start | bytes 1572872 | tf_op jit(solution)/shard_map/ppermute | solution.py:616
  157.7 13.0 %copy-start = (f32[128,2048]{1,0:T(8,128)S(1)}, f32[128,2048]{1,0:T(8,128)}, u32[]{:S(2)}) copy-start(f32[128,2048]{1,0:T(8,128)} %get-tuple-element.24) | copy-start | bytes 3145732

commit v2 on v1

--- a/solution.py
+++ b/solution.py
@@ -46,7 +46,7 @@
                  dx_own, dx_send, dwk_out, dwv_out, wg_out, wu_out, wq_out, wd_out, wo_out,
                  xg, yg, wall, wy, dd, hh, dhs, dob, qs, ks, vs, pb, ds, wqv, wkv, ktmp,
                  dxs, rsend, drecv, rrecv, kvd, kvl, kvr, kvf, kvg, stage,
-                 wsem, ring_s, sib_s, rsem, lsem, gsem, d_s, d_r, r_s, r_r, k_s, k_r, line_s, line_r):
+                 wsem, ring_s, sib_s, rsem, lsem, osem, gsem, d_s, d_r, r_s, r_r, k_s, k_r, line_s, line_r):
     S = z_
     n, chips, tok, pair, d_model, hd = S.n, S.chips, S.tok, S.pair, S.d, S.hd
     sub_rows = tok // SUBS
@@ -89,13 +89,13 @@
     def ring_copy(st, slot, sub, src):
         return pltpu.make_async_remote_copy(
             src_ref=src, dst_ref=gathered[st].at[rows(slot + 1, c, sub)],
-            send_sem=ring_s.at[st, slot, sub], recv_sem=rsem.at[st, slot + 1, c, sub],
+            send_sem=ring_s.at[st], recv_sem=rsem.at[st, slot + 1, c, sub],
             device_id={"tp": nxt}, device_id_type=MESH)
 
     def sib_copy(st, slot, sub, src):
         return pltpu.make_async_remote_copy(
             src_ref=src, dst_ref=gathered[st].at[rows(slot, c, sub)],
-            send_sem=sib_s.at[st, slot, sub], recv_sem=rsem.at[st, slot, c, sub],
+            send_sem=sib_s.at[st], recv_sem=rsem.at[st, slot, c, sub],
             device_id={"tp": sib}, device_id_type=MESH)
 
     def here(st, slot, sub):
@@ -104,7 +104,7 @@
     def wait_block(st, slot, ring, sub):
         ref = gathered[st].at[rows(slot, ring, sub)]
         pltpu.make_async_remote_copy(
-            src_ref=ref, dst_ref=ref, send_sem=ring_s.at[st, 0, sub], recv_sem=rsem.at[st, slot, ring, sub],
+            src_ref=ref, dst_ref=ref, send_sem=ring_s.at[st], recv_sem=rsem.at[st, slot, ring, sub],
             device_id={"tp": sib}, device_id_type=MESH).wait_recv()
 
     def start_ring(st):
@@ -134,8 +134,7 @@
 
     wall[S.at + 2 * ft:S.ak, :] = jnp.zeros((128 - 2 * ft, d_model), BF)
     wy[S.yt + ft:S.yo, :] = jnp.zeros((128 - ft, d_model), BF)
-    for i in (1, 2):
-        stage[i] = jnp.zeros(stage.shape[1:], F32)
+    stage[1] = jnp.zeros(stage.shape[1:], F32)
     rrecv[0] = jnp.zeros(rrecv.shape[1:], BF)
     qcopy.wait()
     kcopy.wait()
@@ -241,7 +240,7 @@
             pump(0, slot + 2, 0)
 
     kc = 256
-    sc, dka, dva = stage.at[0], stage.at[1], stage.at[2]
+    sc, dka, dva = stage.at[0, pl.ds(0, tok)], stage.at[1, pl.ds(0, tok)], stage.at[1, pl.ds(tok, tok)]
 
     def attend(slot, ring, blk, chunks):
         qrow = pl.ds(pl.multiple_of(blk * tok, tok), tok)
@@ -312,6 +311,18 @@
             src_ref=dxs.at[lax.rem(k, 2), pl.ds(pl.multiple_of((1 - c) * tok, tok), tok)], dst_ref=drecv.at[k],
             send_sem=d_s.at[k], recv_sem=d_r.at[k], device_id={"tp": sib}, device_id_type=MESH)
 
+    def dx_main(k, part):
+        at = pl.ds(pl.multiple_of(part * (d_model // 2), 1024), d_model // 2)
+        out = dot_nn(dd[slot_rows(k + 1), 0:S.ak], wall[0:S.ak, at])
+        dxs[k, :, at] = out.astype(BF)
+
+    def dx_kv(k):
+        lhs = dd[slice((k + 1) * pair, (k + 2) * pair), S.ak:S.wa]
+        for nb in range(0, d_model, 512):
+            out = dot_nn(lhs, wall[S.ak:S.wa, nb:nb + 512])
+            dxs[k, :, nb:nb + 512] = (dxs[k, :, nb:nb + 512].astype(F32) + out).astype(BF)
+        d_copy(jnp.int32(k)).start()
+
     def dx_part(k):
         buf = lax.rem(k, 2)
         lhs = dd[slot_rows(lax.rem(k + 1, chips)), :]
@@ -324,6 +335,10 @@
         y_out(slot, c)
         attend_ring(slot, c)
 
+        @pl.when(jnp.logical_and(slot >= 3, slot < 7))
+        def _():
+            dx_main(lax.div(slot - 3, 2), lax.rem(slot - 3, 2))
+
         @pl.when(jnp.logical_and(slot > 0, slot < chips - 1))
         def _():
             pump(1, slot + 1, 0)
@@ -338,7 +353,7 @@
         @pl.when(slot == chips - 1)
         def _():
             kv_own()
-            dx_part(jnp.int32(0))
+            dx_kv(0)
 
         @pl.when(slot > 0)
         def _():
@@ -381,7 +396,7 @@
     def kv_point(p):
         for way in range(2):
             at = place if way == 0 else last_place - place
-            i = p - lag * at
+            i = p + 1 - lag * at
             buf, got = ((ks, kvl), (vs, kvr))[way]
 
             @pl.when(jnp.logical_and(jnp.logical_and(i >= 0, i < parts), at < last_place))
@@ -415,8 +430,7 @@
                 dd[dst, S.av:S.wa] = jnp.where(first_core, kvg[src, :], kvf[src, :])
         own = pl.multiple_of(lax.rem(me, n // S.kv) * dwk_out.shape[1], 128)
         out = dot_tn(xg[:, pl.ds(own, dwk_out.shape[1])], dd[:, S.ak:S.wa])
-        dwk_out[0] = out[:, 0:hd]
-        dwv_out[0] = out[:, hd:2 * hd]
+        dhs[:, 0:2 * hd] = out
 
     def r_copy(k, sub):
         cut_rows = pl.ds(sub * sub_rows, sub_rows)
@@ -451,40 +465,58 @@
         def _():
             r_copy(k, sub).start()
 
-    whole = fm // 128
-    kinds = (
-        (0, whole, ((wg_out, None, 0, 128),)), (whole, 2 * whole, ((wu_out, None, 0, 128),)),
-        (2 * whole, 2 * whole + 1, ((wq_out, 0, 0, 128),)),
-        (2 * whole + 1, 2 * whole + 2, ((wg_out, fm, 0, ft), (wu_out, fm, ft, ft))),
-        (2 * whole + 2, 3 * whole + 2, ((wd_out, None, 0, 128),)), (3 * whole + 2, 3 * whole + 3, ((wd_out, fm, 0, ft),)),
-        (3 * whole + 3, 3 * whole + 4, ((wo_out, 0, 0, 128),)),
+    rows_of = (
+        ((wo_out, 0, 0, hd),),
+        ((wg_out, 0, 0, kc),), ((wg_out, kc, 0, kc),), ((wg_out, 2 * kc, 0, fm - 2 * kc), (wu_out, 0, fm - 2 * kc, 3 * kc - fm)),
+        ((wu_out, 3 * kc - fm, 0, kc),), ((wu_out, 4 * kc - fm, 0, kc),),
+        ((wq_out, 0, 0, hd), (wg_out, fm, hd, ft), (wu_out, fm, hd + ft, ft)),
+        ((wd_out, 0, 0, kc),), ((wd_out, kc, 0, kc),), ((wd_out, 2 * kc, 0, fm - 2 * kc), (wd_out, fm, fm - 2 * kc, ft)),
     )
-    x_units, units = 2 * whole + 2, 3 * whole + 4
-    slots = stage.shape[0]
-
-    def g_do(u, act):
-        for lo, hi, pieces in kinds:
+    units, x_end = len(rows_of), 7
+
+    def g_copies(u):
+        return [pltpu.make_async_copy(stage.at[u % 2, pl.ds(src, size)], ref.at[pl.ds(dst, size)], gsem.at[u % 2, i])
+                for i, (ref, dst, src, size) in enumerate(rows_of[u])]
+
+    def dw_unit(u):
+        for w in range(2, units):
+            @pl.when(u == w)
+            def _():
+                for cp in g_copies(w - 2):
+                    cp.wait()
+        buf = lax.rem(u, 2)
+
+        @pl.when(u == 0)
+        def _():
+            for nb in range(0, d_model, kc):
+                stage[0, 0:hd, nb:nb + kc] = dot_tn(hh[:, S.yo:S.wy], yg[:, nb:nb + kc])
+        for lhs, rhs, lo, hi in ((dd, xg, 1, x_end), (hh, yg, x_end, units)):
             @pl.when(jnp.logical_and(u >= lo, u < hi))
             def _():
-                for i, (ref, dst, src, size) in enumerate(pieces):
-                    row = pl.multiple_of((u - lo) * 128, 128) if dst is None else dst
-                    slot = lax.rem(u, slots)
-                    act(pltpu.make_async_copy(stage.at[slot, pl.ds(src, size)], ref.at[pl.ds(row, size)], gsem.at[slot, i]))
-
-    def dw_unit(u):
-        @pl.when(jnp.logical_and(u >= slots, u < units))
-        def _():
-            g_do(u - slots, lambda cp: cp.wait())
-        slot = lax.rem(u, slots)
-        for lhs, rhs, lo, hi in ((dd, xg, 0, x_units), (hh, yg, x_units, units)):
-            @pl.when(jnp.logical_and(u >= lo, u < hi))
+                at = pl.ds(pl.multiple_of((u - lo) * kc, kc), kc)
+                for nb in range(0, d_model, kc):
+                    stage[buf, :, nb:nb + kc] = dot_tn(lhs[:, at], rhs[:, nb:nb + kc])
+        for w in range(units):
+            @pl.when(u == w)
             def _():
-                at = pl.ds(pl.multiple_of((u - lo) * 128, 128), 128)
-                for nb in range(0, d_model, kc):
-                    stage[slot, :, nb:nb + kc] = dot_tn(lhs[:, at], rhs[:, nb:nb + kc])
-        g_do(u, lambda cp: cp.start())
+                for cp in g_copies(w):
+                    cp.start()
+
+    own_k = chips - 1
+
+    def own_tokens():
+        d_wait(own_k)
+        for g in range(0, tok, 16):
+            mine = dxs[own_k % 2, pl.ds(pl.multiple_of(c * tok + g, 16), 16), :].astype(F32)
+            pb[g:g + 16, :] = (mine + drecv[own_k, g:g + 16, :].astype(F32)).astype(BF)
+
+    last = [pltpu.make_async_copy(pb, dx_own, osem.at[0]),
+            pltpu.make_async_copy(dhs.at[:, pl.ds(0, hd)], dwk_out.at[0], osem.at[1]),
+            pltpu.make_async_copy(dhs.at[:, pl.ds(hd, hd)], dwv_out.at[0], osem.at[2]),
+            pltpu.make_async_copy(rsend.at[(own_k - 1) % 2], dx_send, osem.at[3])]
 
     kv_begin()
+    kv_point(-1)
     kv_point(0)
 
     @pl.loop(0, chips - 1)
@@ -493,33 +525,40 @@
         dx_pump(k, 0)
         kv_point(2 * k + 1)
 
+        @pl.when(k == 0)
+        def _():
+            dx_kv(1)
+
         @pl.when(k >= 1)
         def _():
             d_copy(k - 1).wait_send()
-        dx_part(k + 1)
-
-        dw_unit(3 * k)
+            dx_part(k + 1)
+
+        @pl.when(jnp.logical_and(k >= 2, k < chips - 3))
+        def _():
+            dw_unit(2 * k - 1)
+
+        @pl.when(k == chips - 2)
+        def _():
+            kv_last()
+            last[1].start()
+            last[2].start()
+            own_tokens()
+            last[0].start()
         dx_pump(k, 1)
         kv_point(2 * k + 2)
 
-        @pl.when(k == chips - 2)
+        @pl.loop(0, jnp.where(k == 0, 2, jnp.where(k < chips - 2, 1, 0)))
+        def _(i):
+            dw_unit(jnp.where(k == 0, i, jnp.minimum(2 * k, units - 1)))
+
+        @pl.when(k == chips - 3)
         def _():
             kv_sum()
 
-        @pl.loop(0, 2)
-        def _(i):
-            dw_unit(3 * k + 1 + i)
-
-    own_k = chips - 1
-    dx_copy = pltpu.make_async_copy(rsend.at[(own_k - 1) % 2], dx_send, lsem.at[0])
-    dx_copy.start()
-    d_wait(own_k)
-    buf = own_k % 2
-    for g in range(0, tok, 16):
-        mine = dxs[buf, pl.ds(pl.multiple_of(c * tok + g, 16), 16), :].astype(F32)
-        dx_own[g:g + 16, :] = mine + drecv[own_k, g:g + 16, :].astype(F32)
-    dx_copy.wait()
-    kv_last()
+    last[3].start()
+    for cp in last:
+        cp.wait()
 
     for way in range(2):
         at = place if way == 0 else last_place - place
@@ -533,16 +572,15 @@
     for k in range(chips - 2, chips):
         d_copy(k).wait_send()
 
-    @pl.loop(0, chips)
-    def _(slot):
-        for st in range(2):
-            for sub in range(SUBS):
-                @pl.when(slot < chips - 1)
-                def _():
-                    ring_copy(st, slot, sub, here(st, slot, sub)).wait_send()
-                sib_copy(st, slot, sub, here(st, slot, sub)).wait_send()
-    for u in range(units - slots, units):
-        g_do(jnp.int32(u), lambda cp: cp.wait())
+    for st in range(2):
+        for sem, count in ((ring_s, chips - 1), (sib_s, chips)):
+            span_all = gathered[st].at[pl.ds(0, count * tok)]
+            pltpu.make_async_remote_copy(
+                src_ref=span_all, dst_ref=span_all, send_sem=sem.at[st], recv_sem=rsem.at[st, 0, 0, 0],
+                device_id={"tp": sib}, device_id_type=MESH).wait_send()
+    for u in range(units - 2, units):
+        for cp in g_copies(u):
+            cp.wait()
 
 
 def finish_kernel(wg_hbm, wu_hbm, wd_hbm, wo_hbm, wq_hbm, dwk_hbm, dwv_hbm,
@@ -577,7 +615,6 @@
         S = Sizes(n_dev, kv, tok, d_model, ff, hd)
         seq, chips, pair = S.seq, S.chips, S.pair
         any_spec = pl.BlockSpec(memory_space=pl.ANY)
-        vm = pl.BlockSpec(memory_space=pltpu.VMEM)
         dma = pltpu.SemaphoreType.DMA
         reps = n_dev // kv
         dcut = d_model // reps
@@ -586,12 +623,12 @@
         outs = pl.pallas_call(
             functools.partial(fused_kernel, S),
             out_shape=(
-                jax.ShapeDtypeStruct((tok, d_model), F32),
+                jax.ShapeDtypeStruct((tok, d_model), BF),
                 jax.ShapeDtypeStruct((tok, d_model), BF),
                 kv_out, kv_out, ff_out, ff_out, hd_out, ff_out, hd_out,
             ),
             in_specs=[any_spec] * 9,
-            out_specs=(vm, any_spec, vm, vm) + (any_spec,) * 5,
+            out_specs=[any_spec] * 9,
             scratch_shapes=[
                 pltpu.VMEM((seq, d_model), BF), pltpu.VMEM((seq, d_model), BF),
                 pltpu.VMEM((S.wa, d_model), BF), pltpu.VMEM((S.wy, d_model), BF),
@@ -603,9 +640,9 @@
                 pltpu.VMEM((chips, tok, d_model), BF), pltpu.VMEM((chips, tok, d_model), BF),
                 pltpu.VMEM((seq, hd), BF), pltpu.VMEM((seq, hd), BF), pltpu.VMEM((seq, hd), BF),
                 pltpu.VMEM((seq, hd), BF), pltpu.VMEM((seq, hd), BF),
-                pltpu.VMEM((4, hd, d_model), F32),
-                dma((10,)), dma((2, chips, SUBS)), dma((2, chips, SUBS)), dma((2, chips, 2, SUBS)), dma((2,)),
-                dma((4, 2)), dma((chips,)), dma((chips,)), dma((chips, SUBS)), dma((chips, SUBS)), dma((2,)), dma((2,)),
+                pltpu.VMEM((2, 2 * hd, d_model), F32),
+                dma((10,)), dma((2,)), dma((2,)), dma((2, chips, 2, SUBS)), dma((2,)), dma((4,)),
+                dma((2, 3)), dma((chips,)), dma((chips,)), dma((chips, SUBS)), dma((chips, SUBS)), dma((2,)), dma((2,)),
                 dma((2, KV_PARTS)), dma((2, KV_PARTS)),
             ],
             compiler_params=pltpu.CompilerParams(collective_id=0, has_side_effects=True, vmem_limit_bytes=67043328),
@@ -627,7 +664,7 @@
             compiler_params=pltpu.CompilerParams(vmem_limit_bytes=62 << 20),
             name="finish",
         )(wg, wu, wd, wo, wq, dwk, dwv)
-        dx = (dx_own + dx_last.astype(F32)).astype(BF)
+        dx = (dx_own.astype(F32) + dx_last.astype(F32)).astype(BF)
         return (dx, wq.reshape(d_model, 1, hd), dwk, dwv, wo[None], wg.T, wu.T, wd)
 
     token_spec = P(("dp", "tp"), None)

time: 172 us -> 169 us (0.983)
  Pallas kernels: 168 us -> 165 us
    pallas_call x1, Pallas kernels: 155 us -> 152 us  [local_step(): pl.pallas_call(functools.partial(fused_kernel, S), out_shape=(jax.ShapeDt...]
where the time goes in v2:
time: 169 us
  Pallas kernels  165 us (98%)
  starting transfers between devices  2.39 us (1%)
    pallas_call x1, Pallas kernels, local_step(): pl.pallas_call(functools.partial(fused_kernel, S), out_shape=(jax.ShapeDt...  152 us
    pallas_call x1, Pallas kernels, local_step(): pl.pallas_call(finish_kernel, in_specs=[any_spec] * 7, out_specs=[any_spe...  12.9 us
  transfers between devices with their start and end apart: 1, of which 0 were waited for; matrix products, arithmetic and copies ran while one was open for 0% of the time, Pallas kernels for 8%

profile of v2, /device:TPU:21, one launch (start us, length us, event | category | flops | bytes accessed | tf_op | source)
XLA Modules:
  0.0 168.9 jit_solution(5186034366381600403)
XLA Ops:
  0.6 152.0 %fused.1 = (bf16[128,2048]{1,0:T(8,128)(2,1)}, bf16[128,2048]{1,0:T(8,128)(2,1)}, f32[1,256,128]{2,1,0:T(8,128)}, f32[1,256,128]{2,1,0:T(8,128)}, f32[688,2048]{...) custom-call(bf16[128,2048]{1,0:T(8,128)(2,1)} %x_hbm.1, ...), custom_call_target="tpu_custom_call" | custom-call | tf_op jit(solution)/shard_map/fused/pallas_call | solution.py:623
  152.7 2.4 %collective-permute-start = (bf16[128,2048]{1,0:T(8,128)(2,1)}, bf16[128,2048]{1,0:T(8,128)(2,1)S(1)}, u32[]{:S(2)}, u32[]{:S(2)}) collective-permute-start(bf16[128,2048]{1,0:T(8,128)(2,1)} %get-tuple-element.25), channel_id=1, source_target_pairs={{0,2},{1,15},{2,4},{3,1},{4,6},{5,3},{6,8},{7,5},{8,10},{9,7},{10,... | collective-permute-start | bytes 1572872 | tf_op jit(solution)/shard_map/ppermute | solution.py:653
  155.0 0.0 copy-start
  155.0 12.9 %finish.1 = (f32[688,2048]{1,0:T(8,128)}, f32[688,2048]{1,0:T(8,128)}, f32[688,2048]{1,0:T(8,128)}, f32[128,2048]{1,0:T(8,128)}, f32[2048,128]{1,0:T(8,128)}, /*...) custom-call(f32[688,2048]{1,0:T(8,128)} %get-tuple-element.26.wg_hbm, f32[688,2048]{1,0:T(8,128)} %get-tuple-element.27.wu_hbm, ...), custom_call_target="tpu_custom_call" | custom-call | flops 10000000000 | bytes 38000000 | tf_op jit(solution)/shard_map/finish/pallas_call | solution.py:654
  168.0 0.0 collective-permute-done
  168.0 0.0 copy-done
  168.0 0.9 add_convert_fusion
Async XLA Ops:
  152.7 15.3 %collective-permute-start = (bf16[128,2048]{1,0:T(8,128)(2,1)}, bf16[128,2048]{1,0:T(8,128)(2,1)S(1)}, u32[]{:S(2)}, u32[]{:S(2)}) collective-permute-start(bf16[128,2048]{1,0:T(8,128)(2,1)} %get-tuple-element.25), channel_id=1, source_target_pairs={{0,2},{1,15},{2,4},{3,1},{4,6},{5,3},{6,8},{7,5},{8,10},{9,7},{10,... | collective-permute-start | bytes 1572872 | tf_op jit(solution)/shard_map/ppermute | solution.py:653
  155.0 12.9 %copy-start = (bf16[128,2048]{1,0:T(8,128)(2,1)S(1)}, bf16[128,2048]{1,0:T(8,128)(2,1)}, u32[]{:S(2)}) copy-start(bf16[128,2048]{1,0:T(8,128)(2,1)} %get-tuple-element.24) | copy-start | bytes 1572868

commit v3 on v2

--- a/solution.py
+++ b/solution.py
@@ -358,6 +358,9 @@
         @pl.when(slot > 0)
         def _():
             y_first(slot)
+
+        @pl.when(jnp.logical_and(slot > 0, slot < chips - 1))
+        def _():
             mlp_mid(slot)
 
         @pl.when(slot < chips - 1)
@@ -513,7 +516,9 @@
     last = [pltpu.make_async_copy(pb, dx_own, osem.at[0]),
             pltpu.make_async_copy(dhs.at[:, pl.ds(0, hd)], dwk_out.at[0], osem.at[1]),
             pltpu.make_async_copy(dhs.at[:, pl.ds(hd, hd)], dwv_out.at[0], osem.at[2]),
-            pltpu.make_async_copy(rsend.at[(own_k - 1) % 2], dx_send, osem.at[3])]
+            pltpu.make_async_copy(rsend.at[(own_k - 1) % 2, pl.ds(0, sub_rows)], dx_send.at[pl.ds(0, sub_rows)], osem.at[4]),
+            pltpu.make_async_copy(rsend.at[(own_k - 1) % 2, pl.ds(sub_rows, sub_rows)], dx_send.at[pl.ds(sub_rows, sub_rows)],
+                                  osem.at[3])]
 
     kv_begin()
     kv_point(-1)
@@ -528,6 +533,7 @@
         @pl.when(k == 0)
         def _():
             dx_kv(1)
+            mlp_mid(chips - 1)
 
         @pl.when(k >= 1)
         def _():
@@ -540,6 +546,7 @@
 
         @pl.when(k == chips - 2)
         def _():
+            last[3].start()
             kv_last()
             last[1].start()
             last[2].start()
@@ -556,7 +563,7 @@
         def _():
             kv_sum()
 
-    last[3].start()
+    last[4].start()
     for cp in last:
         cp.wait()
 
@@ -641,7 +648,7 @@
                 pltpu.VMEM((seq, hd), BF), pltpu.VMEM((seq, hd), BF), pltpu.VMEM((seq, hd), BF),
                 pltpu.VMEM((seq, hd), BF), pltpu.VMEM((seq, hd), BF),
                 pltpu.VMEM((2, 2 * hd, d_model), F32),
-                dma((10,)), dma((2,)), dma((2,)), dma((2, chips, 2, SUBS)), dma((2,)), dma((4,)),
+                dma((10,)), dma((2,)), dma((2,)), dma((2, chips, 2, SUBS)), dma((2,)), dma((5,)),
                 dma((2, 3)), dma((chips,)), dma((chips,)), dma((chips, SUBS)), dma((chips, SUBS)), dma((2,)), dma((2,)),
                 dma((2, KV_PARTS)), dma((2, KV_PARTS)),
             ],

time: 169 us -> 168 us (level)
  no operation moved by 1% of the time
where the time goes in v3:
time: 168 us
  Pallas kernels  164 us (98%)
  starting transfers between devices  2.81 us (2%)
    pallas_call x1, Pallas kernels, local_step(): pl.pallas_call(functools.partial(fused_kernel, S), out_shape=(jax.ShapeDt...  151 us
    pallas_call x1, Pallas kernels, local_step(): pl.pallas_call(finish_kernel, in_specs=[any_spec] * 7, out_specs=[any_spe...  12.9 us
  transfers between devices with their start and end apart: 1, of which 0 were waited for; matrix products, arithmetic and copies ran while one was open for 0% of the time, Pallas kernels for 8%

profile of v3, /device:TPU:21, one launch (start us, length us, event | category | flops | bytes accessed | tf_op | source)
XLA Modules:
  0.0 168.3 jit_solution(7498028796864727865)
XLA Ops:
  0.6 150.9 %fused.1 = (bf16[128,2048]{1,0:T(8,128)(2,1)}, bf16[128,2048]{1,0:T(8,128)(2,1)}, f32[1,256,128]{2,1,0:T(8,128)}, f32[1,256,128]{2,1,0:T(8,128)}, f32[688,2048]{...) custom-call(bf16[128,2048]{1,0:T(8,128)(2,1)} %x_hbm.1, ...), custom_call_target="tpu_custom_call" | custom-call | tf_op jit(solution)/shard_map/fused/pallas_call | solution.py:630
  151.6 2.8 %collective-permute-start = (bf16[128,2048]{1,0:T(8,128)(2,1)}, bf16[128,2048]{1,0:T(8,128)(2,1)S(1)}, u32[]{:S(2)}, u32[]{:S(2)}) collective-permute-start(bf16[128,2048]{1,0:T(8,128)(2,1)} %get-tuple-element.25), channel_id=1, source_target_pairs={{0,2},{1,15},{2,4},{3,1},{4,6},{5,3},{6,8},{7,5},{8,10},{9,7},{10,... | collective-permute-start | bytes 1572872 | tf_op jit(solution)/shard_map/ppermute | solution.py:660
  154.4 0.0 copy-start
  154.4 12.9 %finish.1 = (f32[688,2048]{1,0:T(8,128)}, f32[688,2048]{1,0:T(8,128)}, f32[688,2048]{1,0:T(8,128)}, f32[128,2048]{1,0:T(8,128)}, f32[2048,128]{1,0:T(8,128)}, /*...) custom-call(f32[688,2048]{1,0:T(8,128)} %get-tuple-element.26.wg_hbm, f32[688,2048]{1,0:T(8,128)} %get-tuple-element.27.wu_hbm, ...), custom_call_target="tpu_custom_call" | custom-call | flops 10000000000 | bytes 38000000 | tf_op jit(solution)/shard_map/finish/pallas_call | solution.py:661
  167.3 0.0 collective-permute-done
  167.3 0.0 copy-done
  167.3 0.9 add_convert_fusion
Async XLA Ops:
  151.6 15.7 %collective-permute-start = (bf16[128,2048]{1,0:T(8,128)(2,1)}, bf16[128,2048]{1,0:T(8,128)(2,1)S(1)}, u32[]{:S(2)}, u32[]{:S(2)}) collective-permute-start(bf16[128,2048]{1,0:T(8,128)(2,1)} %get-tuple-element.25), channel_id=1, source_target_pairs={{0,2},{1,15},{2,4},{3,1},{4,6},{5,3},{6,8},{7,5},{8,10},{9,7},{10,... | collective-permute-start | bytes 1572872 | tf_op jit(solution)/shard_map/ppermute | solution.py:660
  154.4 12.9 %copy-start = (bf16[128,2048]{1,0:T(8,128)(2,1)S(1)}, bf16[128,2048]{1,0:T(8,128)(2,1)}, u32[]{:S(2)}) copy-start(bf16[128,2048]{1,0:T(8,128)(2,1)} %get-tuple-element.24) | copy-start | bytes 1572868
